TPU v7x, 32 devices: a whole 2x2x4 slice. The times are simulated.
32 devices in a mesh: rep: 8 (over y, x, core), tp: 4 (over z).
Axes of the slice: x: 2, y: 2, z: 4, core: 2. Of those that a mesh axis runs over, the one named last changes fastest.
Arguments:
- tokens: bfloat16 [4096, 8192], P('rep'), may hold values from -6 to 6
- query_weight: float32 [8192, 8192], P(('rep', 'tp')), may hold values from -0.0625 to 0.0625
- key_weight: float32 [8192, 1024], P(('rep', 'tp')), may hold values from -0.0625 to 0.0625
- value_weight: float32 [8192, 1024], P(('rep', 'tp')), may hold values from -0.0625 to 0.0625
- cache_keys: bfloat16 [256, 128, 1024], P('rep', None, 'tp'), may hold values from -240 to 240
- cache_values: bfloat16 [256, 128, 1024], P('rep', None, 'tp'), may hold values from -6 to 6
- lengths: int32 [8, 2], P('rep'), may hold values from 1 to 2048
- page_table: int32 [8, 2, 16], P('rep'), may hold values from 0 to 31, as said below
Outputs:
- attended: bfloat16 [4096, 8192], P('rep', 'tp')
- new_cache: bfloat16 [2, 4096, 1024], P(None, 'rep', 'tp')
Inputs may be any that keep to these rules, and one draw needn't show every extreme that they name: For each group g, the 2 x 16 entries of page_table[g] name each of the group's local pool pages 0 to 31 exactly once.
All inputs are finite; a program needn't handle non-finite values.
Results may differ from a plain program's by a relative error of at most 0.008.
The roundings to bfloat16 on the way count: a program that leaves them out, or rounds other values in their place, can miss the bound.
Values may be sent and summed in bfloat16 or wider, within the bound.
A program may use at most 192 MiB of HBM per device.

v0:
```python
import jax
import jax.numpy as jnp
from jax import lax
from jax.sharding import PartitionSpec as P

HEADS = 64
KV_HEADS = 8
HEAD_DIM = 128
SEQS = 2
NEW = 256
TOK = 512
MAXLEN = 2048
ROPE_THETA = 500000.0


def rotate(vectors, positions):
    half_dim = HEAD_DIM // 2
    frequency = ROPE_THETA ** (-2.0 * jnp.arange(half_dim, dtype=jnp.float32) / HEAD_DIM)
    angles = positions.astype(jnp.float32)[:, None] * frequency[None, :]
    cosine_part = jnp.cos(angles)[:, None, :]
    sine_part = jnp.sin(angles)[:, None, :]
    first_half = vectors[..., :half_dim]
    second_half = vectors[..., half_dim:]
    return jnp.concatenate(
        [
            first_half * cosine_part - second_half * sine_part,
            second_half * cosine_part + first_half * sine_part,
        ],
        axis=-1,
    )


def per_device(
    tokens, query_weight, key_weight, value_weight, cache_keys, cache_values, lengths, page_table
):
    weights = (
        query_weight.astype(jnp.bfloat16),
        key_weight.astype(jnp.bfloat16),
        value_weight.astype(jnp.bfloat16),
    )
    slabs = (
        lax.all_to_all(weights[0], "tp", split_axis=1, concat_axis=0, tiled=True),
        lax.all_to_all(weights[1], "tp", split_axis=1, concat_axis=0, tiled=True),
        lax.all_to_all(weights[2], "tp", split_axis=1, concat_axis=0, tiled=True),
    )
    pieces = (
        lax.all_gather(slabs[0], "rep", axis=0, tiled=True),
        lax.all_gather(slabs[1], "rep", axis=0, tiled=True),
        lax.all_gather(slabs[2], "rep", axis=0, tiled=True),
    )
    raw_query, raw_key, raw_value = tuple(
        (jnp.dot(tokens, piece, preferred_element_type=jnp.float32) for piece in pieces)
    )
    kv_local = raw_key.shape[1] // HEAD_DIM
    group_size = HEADS // KV_HEADS
    scale = 1.0 / HEAD_DIM**0.5
    seq_lengths = lengths[0]
    positions = (seq_lengths[:, None] + jnp.arange(NEW, dtype=jnp.int32)[None, :]).reshape(TOK)
    queries = rotate(raw_query.reshape(TOK, kv_local * group_size, HEAD_DIM), positions).astype(
        jnp.bfloat16
    )
    new_keys = rotate(raw_key.reshape(TOK, kv_local, HEAD_DIM), positions).astype(jnp.bfloat16)
    new_values = raw_value.astype(jnp.bfloat16).reshape(TOK, kv_local, HEAD_DIM)

    def one_sequence(inner):
        seq_queries, seq_keys, seq_values, page_rows, length = inner
        old_keys = cache_keys[page_rows].reshape(MAXLEN, kv_local, HEAD_DIM)
        old_values = cache_values[page_rows].reshape(MAXLEN, kv_local, HEAD_DIM)
        all_keys = jnp.concatenate([old_keys, seq_keys], axis=0)
        all_values = jnp.concatenate([old_values, seq_values], axis=0)
        grouped = seq_queries.reshape(NEW, kv_local, group_size, HEAD_DIM)
        scores = (
            jnp.einsum("nkgd,mkd->kgnm", grouped, all_keys, preferred_element_type=jnp.float32)
            * scale
        )
        key_index = jnp.arange(MAXLEN + NEW, dtype=jnp.int32)[None, :]
        query_index = jnp.arange(NEW, dtype=jnp.int32)[:, None]
        visible = jnp.where(
            key_index < MAXLEN, key_index < length, key_index - MAXLEN <= query_index
        )
        scores = jnp.where(visible[None, None], scores, -1e30)
        maxima = jnp.max(scores, axis=-1, keepdims=True)
        expons = jnp.exp(scores - maxima)
        probs = (expons / jnp.sum(expons, axis=-1, keepdims=True)).astype(jnp.bfloat16)
        output = jnp.einsum("kgnm,mkd->nkgd", probs, all_values, preferred_element_type=jnp.float32)
        return output.astype(jnp.bfloat16).reshape(NEW, kv_local * group_size * HEAD_DIM)

    attended = lax.map(
        one_sequence,
        (
            queries.reshape(SEQS, NEW, kv_local * group_size, HEAD_DIM),
            new_keys.reshape(SEQS, NEW, kv_local, HEAD_DIM),
            new_values.reshape(SEQS, NEW, kv_local, HEAD_DIM),
            page_table[0],
            seq_lengths,
        ),
    )
    new_cache = jnp.stack(
        [new_keys.reshape(TOK, kv_local * HEAD_DIM), new_values.reshape(TOK, kv_local * HEAD_DIM)]
    )
    return (attended.reshape(TOK, kv_local * group_size * HEAD_DIM), new_cache)


def solution(mesh):
    return jax.shard_map(
        per_device,
        mesh=mesh,
        in_specs=(
            P("rep", None),
            P(("rep", "tp"), None),
            P(("rep", "tp"), None),
            P(("rep", "tp"), None),
            P("rep", None, "tp"),
            P("rep", None, "tp"),
            P("rep", None),
            P("rep", None, None),
        ),
        out_specs=(P("rep", "tp"), P(None, "rep", "tp")),
        check_vma=False,
    )
```

profile of v0, /device:TPU:0, one launch (start us, length us, event | category | flops | bytes accessed | tf_op | source)
XLA Modules:
  0.0 450.6 jit_solution(10481622972108164320)
XLA Ops:
  7.2 1.5 copy.33
  8.7 20.6 %all_to_all.57 = bf16[256,4,256]{0,2,1:T(8,128)(2,1)S(1)} all-to-all(bf16[256,4,256]{0,2,1:T(8,128)(2,1)S(1)} %bitcast.110), channel_id=1, replica_groups=mesh['rep'=8,'tp'=4] {'tp'}, dimensions={1} | all-to-all | bytes 1048576 | tf_op jit(solution)/shard_map/all_to_all | solution.py:43
  29.4 1.0 copy.34
  30.7 16.6 %all_to_all.58 = bf16[256,4,256]{0,2,1:T(8,128)(2,1)S(1)} all-to-all(bf16[256,4,256]{0,2,1:T(8,128)(2,1)S(1)} %bitcast.111), channel_id=1, replica_groups=mesh['rep'=8,'tp'=4] {'tp'}, dimensions={1} | all-to-all | bytes 1048576 | tf_op jit(solution)/shard_map/all_to_all | solution.py:44
  47.3 1.0 copy.32
  48.3 7.6 %copy.35 = bf16[256,8192]{0,1:T(8,128)(2,1)} copy(f32[256,8192]{1,0:T(8,128)} %param.11) | data formatting | bytes 12582912 | tf_op args[1]
  55.9 97.8 %all_to_all.59 = bf16[256,4,2048]{0,2,1:T(8,128)(2,1)} all-to-all(bf16[256,4,2048]{0,2,1:T(8,128)(2,1)} %bitcast.105), channel_id=1, replica_groups=mesh['rep'=8,'tp'=4] {'tp'}, dimensions={1} | all-to-all | bytes 8388608 | tf_op jit(solution)/shard_map/all_to_all | solution.py:42
  153.8 6.3 %copy.36 = bf16[4,256,2048]{2,1,0:T(8,128)(2,1)} copy(bf16[4,256,2048]{1,2,0:T(8,128)(2,1)} %bitcast.107) | data formatting | bytes 8388608 | tf_op jit(solution)/shard_map/all_to_all | solution.py:42
  161.4 7.1 %fusion.23 = f32[512,256]{0,1:T(8,128)S(1)} fusion(bf16[512,8192]{1,0:T(8,128)(2,1)} %param.10, bf16[8192,256]{1,0:T(8,128)(2,1)} %all-gather.6.cloned.1.call-done), kind=kOutput, calls=%fused_computation.51 | convolution fusion | flops 2147483648 | bytes 13107200 | tf_op jit(solution)/shard_map/dot_general | solution.py:52
  169.2 9.0 %convolution_convert_fusion = bf16[512,256]{1,0:T(8,128)(2,1)S(1)} fusion(bf16[512,8192]{1,0:T(8,128)(2,1)} %param.10, bf16[8192,256]{1,0:T(8,128)(2,1)} %all-gather.4.cloned.1.call-done), kind=kOutput, calls=%fused_computation.40 | convolution fusion | flops 2147614720 | bytes 12845056 | tf_op jit(solution)/shard_map/dot_general | solution.py:52
  179.2 0.8 pad_maximum_fusion.1
  180.0 140.0 %all-gather.8.cloned.1.call-done = bf16[8192,2048]{1,0:T(8,128)(2,1)} async-done(((bf16[1024,2048]{1,0:T(8,128)(2,1)}), bf16[8192,2048]{1,0:T(8,128)(2,1)}) %all-gather.8.cloned.1.call-update) | async-done | bytes 33554448 | tf_op jit(solution)/shard_map/all_gather | solution.py:47
  320.0 25.8 %fusion.24 = f32[512,2048]{0,1:T(8,128)} fusion(bf16[512,8192]{1,0:T(8,128)(2,1)} %param.10, bf16[8192,2048]{1,0:T(8,128)(2,1)} %all-gather.8.cloned.1.call-done), kind=kOutput, calls=%fused_computation.52 | convolution fusion | flops 17179869184 | bytes 46137344 | tf_op jit(solution)/shard_map/reshape | solution.py:59
  345.8 2.9 subtract_convert_fusion
  349.0 1.1 concatenate.37
  350.2 3.9 pad_maximum_fusion
  354.1 3.7 copy.41
  357.8 86.2 %while.12 = (s32[]{:T(128)}, bf16[2,256,2048]{2,1,0:T(8,128)(2,1)}, s32[2,16]{1,0:T(2,128)S(1)}, bf16[32,128,256]{2,1,0:T(8,128)(2,1)}, bf16[2,256,2,128]{3,2,1,...) while((s32[]{:T(128)}, bf16[2,256,2048]{2,1,0:T(8,128)(2,1)}, ...), condition=%wide.region_3.4_spmd, body=%wide.region_0.3_spmd.sunk | while | flops 4894894080 | bytes 100859848 | solution.py:88
  359.1 1.9 fusion.39
  361.0 2.2 gather_fusion
  363.7 1.3 constant_dynamic-slice_fusion.5
  365.0 17.5 %fusion.41 = (f32[2,8,256]{2,1,0:T(8,128)S(1)}, f32[2,8,256,2304]{2,3,1,0:T(8,128)}) fusion(bf16[256,2,8,128]{3,0,2,1:T(8,128)(2,1)S(1)} %bitcast.103, pred[256,2304]{0,1:T(8,128)(4,1)S(1)} %fusion.39, bf16[256,2,128]{2,0,1:T(8,128)(2,1)S(1)} %dynamic-slice_bitcast_fusion.2, bf16[2048,2,128]{2,0,1:T(8,128)(2,1)S(1)} %copy.60), kind=kOutput, calls=%fused_computation.50.clone.1 | convolution fusion | flops 2456029440 | bytes 40583168 | tf_op jit(solution)/shard_map/while/body/eval_jaxpr/sub | solution.py:83
  382.4 2.2 gather_fusion.1
  386.0 13.3 %fusion.42 = bf16[2,128,8,256]{3,1,2,0:T(8,128)(2,1)S(1)} fusion(f32[2,8,256,2304]{2,3,1,0:T(8,128)} %get-tuple-element.232, f32[2,8,256]{2,1,0:T(8,128)S(1)} %get-tuple-element.233, bf16[256,2,128]{0,2,1:T(8,128)(2,1)S(1)} %bitcast.109, bf16[2048,2,128]{0,2,1:T(8,128)(2,1)S(1)} %copy.62), kind=kOutput, calls=%fused_computation.14.clone.1 | convolution fusion | flops 2437677056 | bytes 39993344 | tf_op jit(solution)/shard_map/while/body/eval_jaxpr/kgnm,mkd->nkgd/dot_general | solution.py:85
  399.9 1.0 constant_dynamic-update-slice_fusion.2
  402.2 1.9 fusion.39
  404.1 2.2 gather_fusion
  406.8 1.3 constant_dynamic-slice_fusion.5
  408.1 17.5 %fusion.41 = (f32[2,8,256]{2,1,0:T(8,128)S(1)}, f32[2,8,256,2304]{2,3,1,0:T(8,128)}) fusion(bf16[256,2,8,128]{3,0,2,1:T(8,128)(2,1)S(1)} %bitcast.103, pred[256,2304]{0,1:T(8,128)(4,1)S(1)} %fusion.39, bf16[256,2,128]{2,0,1:T(8,128)(2,1)S(1)} %dynamic-slice_bitcast_fusion.2, bf16[2048,2,128]{2,0,1:T(8,128)(2,1)S(1)} %copy.60), kind=kOutput, calls=%fused_computation.50.clone.1 | convolution fusion | flops 2456029440 | bytes 40583168 | tf_op jit(solution)/shard_map/while/body/eval_jaxpr/sub | solution.py:83
  425.6 2.2 gather_fusion.1
  429.1 13.3 %fusion.42 = bf16[2,128,8,256]{3,1,2,0:T(8,128)(2,1)S(1)} fusion(f32[2,8,256,2304]{2,3,1,0:T(8,128)} %get-tuple-element.232, f32[2,8,256]{2,1,0:T(8,128)S(1)} %get-tuple-element.233, bf16[256,2,128]{0,2,1:T(8,128)(2,1)S(1)} %bitcast.109, bf16[2048,2,128]{0,2,1:T(8,128)(2,1)S(1)} %copy.62), kind=kOutput, calls=%fused_computation.14.clone.1 | convolution fusion | flops 2437677056 | bytes 39993344 | tf_op jit(solution)/shard_map/while/body/eval_jaxpr/kgnm,mkd->nkgd/dot_general | solution.py:85
  443.0 1.0 constant_dynamic-update-slice_fusion.2
  (57 shorter events, 10.9 us)
Async XLA Ops:
  7.2 23.3 %copy-start.1 = (f32[256,1024]{1,0:T(8,128)S(1)}, f32[256,1024]{1,0:T(8,128)}, u32[]{:S(2)}) copy-start(f32[256,1024]{1,0:T(8,128)} %param.13) | copy-start | bytes 3145732
  7.2 154.2 %all-gather.6.cloned.1.call-start = ((), (), s32[]{:S(2)}) async-start(), calls=%async_computation.4 | async-start | bytes 4718592 | tf_op jit(solution)/shard_map/all_gather | solution.py:48
  30.4 138.8 %all-gather.4.cloned.1.call-start = ((), (), s32[]{:S(2)}) async-start(), calls=%async_computation.3 | async-start | bytes 4718592 | tf_op jit(solution)/shard_map/all_gather | solution.py:49
  48.3 271.8 %all-gather.8.cloned.1.call-start = ((), (), s32[]{:S(2)}) async-start(), calls=%async_computation.5 | async-start | bytes 37748736 | tf_op jit(solution)/shard_map/all_gather | solution.py:47
  160.0 0.7 copy-start.2
  350.2 7.7 %copy-start.3 = (s32[1,2,16]{2,1,0:T(2,128)S(1)}, s32[1,2,16]{2,1,0:T(2,128)}, u32[]{:S(2)}) copy-start(s32[1,2,16]{2,1,0:T(2,128)} %param.17) | copy-start | bytes 388
  354.1 3.7 copy-start
Sparse Core Ops, SparseCore 0:
  30.5 35.6 all-gather.5
  68.7 36.5 all-gather.3
  160.2 159.7 all-gather.7
where the time goes:
time: 451 us
  waiting for transfers between devices  140 us (31%)
  blocking collectives  135 us (30%)
  matrix products  103 us (23%)
  local copies, waits for them, and re-layouts  44 us (10%)
  between operations  13.9 us (3%)
  other arithmetic  13.8 us (3%)
    all_gather x1, waiting for transfers between devices, per_device(): lax.all_gather(slabs[0], 'rep', axis=0, tiled=True)  140 us
    all_to_all x1, blocking collectives, per_device(): lax.all_to_all(weights[0], 'tp', split_axis=1, concat_axis=0, tiled=True)  97.8 us
    sub x2, matrix products, one_sequence(): expons = jnp.exp(scores - maxima)  34.9 us
    dot_general x2, matrix products, one_sequence(): jnp.einsum('kgnm,mkd->nkgd', probs, all_values, preferred_element_type=jn...  26.5 us
    reshape x1, matrix products, per_device(): raw_query.reshape(TOK, kv_local * group_size, HEAD_DIM)  25.8 us
    all_to_all x1, blocking collectives, per_device(): lax.all_to_all(weights[1], 'tp', split_axis=1, concat_axis=0, tiled=True)  20.6 us
    all_to_all x1, blocking collectives, per_device(): lax.all_to_all(weights[2], 'tp', split_axis=1, concat_axis=0, tiled=True)  16.6 us
    dot_general x2, matrix products, per_device(): jnp.dot(tokens, piece, preferred_element_type=jnp.float32)  16.1 us
  transfers between devices with their start and end apart: 3, of which 1 were waited for; matrix products, arithmetic and copies ran while one was open for 8% of the time, Pallas kernels for 0%

commit v1 on v0

--- a/solution.py
+++ b/solution.py
@@ -11,6 +11,13 @@
 TOK = 512
 MAXLEN = 2048
 ROPE_THETA = 500000.0
+
+
+def exchange_blocks(x, mesh_axis, split, join):
+    n_dev = lax.axis_size(mesh_axis)
+    blocks = jnp.stack(jnp.split(x, n_dev, axis=split), axis=0)
+    blocks = lax.all_to_all(blocks, mesh_axis, split_axis=0, concat_axis=0)
+    return jnp.concatenate(blocks, axis=join)
 
 
 def rotate(vectors, positions):
@@ -39,7 +46,7 @@
         value_weight.astype(jnp.bfloat16),
     )
     slabs = (
-        lax.all_to_all(weights[0], "tp", split_axis=1, concat_axis=0, tiled=True),
+        exchange_blocks(weights[0], "tp", 1, 0),
         lax.all_to_all(weights[1], "tp", split_axis=1, concat_axis=0, tiled=True),
         lax.all_to_all(weights[2], "tp", split_axis=1, concat_axis=0, tiled=True),
     )

time: 451 us -> 436 us (0.967)
  local copies, waits for them, and re-layouts: 44 us -> 30.4 us
    reshape x1 -> x0, matrix products: 25.8 us -> none  [per_device(): raw_query.reshape(TOK, kv_local * group_size, HEAD_DIM)]
    dot_general x2 -> x3, matrix products: 16.1 us -> 40.2 us  [per_device(): jnp.dot(tokens, piece, preferred_element_type=jnp.float32)]
    unnamed x12 -> x11, local copies, waits for them, and re-layouts: 9.93 us -> 2.35 us
    all_to_all x1 -> x0, local copies, waits for them, and re-layouts: 6.28 us -> none  [per_device(): lax.all_to_all(weights[0], 'tp', split_axis=1, concat_axis=0, tiled=True)]
  transfers between devices with their start and end apart: 3 -> 3, of which waited for: 1 -> 1; matrix products, arithmetic and copies ran while one was open for 8% -> 6% of each run, Pallas kernels for 0% -> 0%
where the time goes in v1:
time: 436 us; the launch traced here: 435 us
  waiting for transfers between devices  140 us (32%)
  blocking collectives  133 us (31%)
  matrix products  102 us (23%)
  local copies, waits for them, and re-layouts  30.4 us (7%)
  other arithmetic  16.3 us (4%)
  between operations  13.9 us (3%)
    all_gather x1, waiting for transfers between devices, per_device(): lax.all_gather(slabs[0], 'rep', axis=0, tiled=True)  140 us
    all_to_all x1, blocking collectives, exchange_blocks(): blocks = lax.all_to_all(blocks, mesh_axis, split_axis=0, concat_axis=0)  95.4 us
    dot_general x3, matrix products, per_device(): jnp.dot(tokens, piece, preferred_element_type=jnp.float32)  40.2 us
    sub x2, matrix products, one_sequence(): expons = jnp.exp(scores - maxima)  34.9 us
    dot_general x2, matrix products, one_sequence(): jnp.einsum('kgnm,mkd->nkgd', probs, all_values, preferred_element_type=jn...  26.5 us
    all_to_all x1, blocking collectives, per_device(): lax.all_to_all(weights[1], 'tp', split_axis=1, concat_axis=0, tiled=True)  20.6 us
    all_to_all x1, blocking collectives, per_device(): lax.all_to_all(weights[2], 'tp', split_axis=1, concat_axis=0, tiled=True)  16.6 us
  transfers between devices with their start and end apart: 3, of which 1 were waited for; matrix products, arithmetic and copies ran while one was open for 6% of the time, Pallas kernels for 0%

profile of v1, /device:TPU:0, one launch (start us, length us, event | category | flops | bytes accessed | tf_op | source)
XLA Modules:
  0.0 435.2 jit_solution(7797684527547986202)
XLA Ops:
  7.2 1.5 copy.33
  8.7 20.6 %all_to_all.43 = bf16[256,4,256]{0,2,1:T(8,128)(2,1)S(1)} all-to-all(bf16[256,4,256]{0,2,1:T(8,128)(2,1)S(1)} %bitcast.116), channel_id=1, replica_groups=mesh['rep'=8,'tp'=4] {'tp'}, dimensions={1} | all-to-all | bytes 1048576 | tf_op jit(solution)/shard_map/all_to_all | solution.py:50
  29.4 1.0 copy.34
  30.7 16.6 %all_to_all.44 = bf16[256,4,256]{0,2,1:T(8,128)(2,1)S(1)} all-to-all(bf16[256,4,256]{0,2,1:T(8,128)(2,1)S(1)} %bitcast.117), channel_id=1, replica_groups=mesh['rep'=8,'tp'=4] {'tp'}, dimensions={1} | all-to-all | bytes 1048576 | tf_op jit(solution)/shard_map/all_to_all | solution.py:51
  47.3 1.0 copy.32
  48.3 4.2 convert_element_type.57
  53.4 95.4 %all_to_all.45 = bf16[4,256,2048]{2,1,0:T(8,128)(2,1)} all-to-all(bf16[4,256,2048]{2,1,0:T(8,128)(2,1)S(1)} %pad_maximum_fusion), channel_id=1, replica_groups=mesh['rep'=8,'tp'=4] {'tp'}, dimensions={0} | all-to-all | bytes 8388608 | tf_op jit(solution)/shard_map/all_to_all | solution.py:19
  150.1 7.2 %fusion.23 = f32[512,256]{0,1:T(8,128)S(1)} fusion(bf16[512,8192]{1,0:T(8,128)(2,1)} %param.10, bf16[8192,256]{1,0:T(8,128)(2,1)} %all-gather.6.cloned.1.call-done), kind=kOutput, calls=%fused_computation.56 | convolution fusion | flops 2147483648 | bytes 13107200 | tf_op jit(solution)/shard_map/dot_general | solution.py:59
  158.1 9.0 %convolution_convert_fusion = bf16[512,256]{1,0:T(8,128)(2,1)S(1)} fusion(bf16[512,8192]{1,0:T(8,128)(2,1)} %param.10, bf16[8192,256]{1,0:T(8,128)(2,1)} %all-gather.4.cloned.1.call-done), kind=kOutput, calls=%fused_computation.41 | convolution fusion | flops 2147614720 | bytes 12845056 | tf_op jit(solution)/shard_map/dot_general | solution.py:59
  168.1 0.8 pad_maximum_fusion.2
  168.9 139.8 %all-gather.8.cloned.1.call-done = bf16[8192,2048]{1,0:T(8,128)(2,1)} async-done(((bf16[1024,2048]{1,0:T(8,128)(2,1)}), bf16[8192,2048]{1,0:T(8,128)(2,1)}) %all-gather.8.cloned.1.call-update) | async-done | bytes 33554448 | tf_op jit(solution)/shard_map/all_gather | solution.py:54
  308.7 24.0 %fusion.24 = f32[2048,512]{1,0:T(8,128)S(1)} fusion(bf16[8192,2048]{1,0:T(8,128)(2,1)} %all-gather.8.cloned.1.call-done, bf16[512,8192]{1,0:T(8,128)(2,1)} %param.10), kind=kOutput, calls=%fused_computation.57 | convolution fusion | flops 17179869184 | bytes 46137344 | tf_op jit(solution)/shard_map/dot_general | solution.py:59
  333.8 1.1 concatenate.37
  334.9 3.9 pad_maximum_fusion.1
  338.9 3.7 copy.37
  342.6 86.1 %while.12 = (s32[]{:T(128)}, bf16[2,256,2048]{2,1,0:T(8,128)(2,1)}, s32[2,16]{1,0:T(2,128)S(1)}, bf16[32,128,256]{2,1,0:T(8,128)(2,1)}, bf16[2,256,2,128]{3,2,1,...) while((s32[]{:T(128)}, bf16[2,256,2048]{2,1,0:T(8,128)(2,1)}, ...), condition=%wide.region_3.4_spmd, body=%wide.region_0.3_spmd.sunk | while | flops 4894894080 | bytes 100859848 | solution.py:95
  343.8 1.9 fusion.39
  345.7 2.2 gather_fusion
  348.3 1.3 constant_dynamic-slice_fusion.5
  349.7 17.5 %fusion.41 = (f32[2,8,256]{2,1,0:T(8,128)S(1)}, f32[2,8,256,2304]{2,3,1,0:T(8,128)}) fusion(bf16[256,2,8,128]{3,0,2,1:T(8,128)(2,1)S(1)} %bitcast.111, pred[256,2304]{0,1:T(8,128)(4,1)S(1)} %fusion.39, bf16[256,2,128]{2,0,1:T(8,128)(2,1)S(1)} %dynamic-slice_bitcast_fusion.2, bf16[2048,2,128]{2,0,1:T(8,128)(2,1)S(1)} %copy.55), kind=kOutput, calls=%fused_computation.55.clone.1 | convolution fusion | flops 2456029440 | bytes 40583168 | tf_op jit(solution)/shard_map/while/body/eval_jaxpr/sub | solution.py:90
  367.1 2.2 gather_fusion.1
  369.6 0.8 copy.57
  370.7 13.3 %fusion.42 = bf16[2,128,8,256]{3,1,2,0:T(8,128)(2,1)S(1)} fusion(f32[2,8,256,2304]{2,3,1,0:T(8,128)} %get-tuple-element.236, f32[2,8,256]{2,1,0:T(8,128)S(1)} %get-tuple-element.237, bf16[256,2,128]{0,2,1:T(8,128)(2,1)S(1)} %bitcast.115, bf16[2048,2,128]{0,2,1:T(8,128)(2,1)S(1)} %copy.57), kind=kOutput, calls=%fused_computation.14.clone.1 | convolution fusion | flops 2437677056 | bytes 39993344 | tf_op jit(solution)/shard_map/while/body/eval_jaxpr/kgnm,mkd->nkgd/dot_general | solution.py:92
  384.6 1.0 constant_dynamic-update-slice_fusion.2
  386.8 1.9 fusion.39
  388.7 2.2 gather_fusion
  391.4 1.3 constant_dynamic-slice_fusion.5
  392.7 17.5 %fusion.41 = (f32[2,8,256]{2,1,0:T(8,128)S(1)}, f32[2,8,256,2304]{2,3,1,0:T(8,128)}) fusion(bf16[256,2,8,128]{3,0,2,1:T(8,128)(2,1)S(1)} %bitcast.111, pred[256,2304]{0,1:T(8,128)(4,1)S(1)} %fusion.39, bf16[256,2,128]{2,0,1:T(8,128)(2,1)S(1)} %dynamic-slice_bitcast_fusion.2, bf16[2048,2,128]{2,0,1:T(8,128)(2,1)S(1)} %copy.55), kind=kOutput, calls=%fused_computation.55.clone.1 | convolution fusion | flops 2456029440 | bytes 40583168 | tf_op jit(solution)/shard_map/while/body/eval_jaxpr/sub | solution.py:90
  410.2 2.2 gather_fusion.1
  412.7 0.8 copy.57
  413.7 13.3 %fusion.42 = bf16[2,128,8,256]{3,1,2,0:T(8,128)(2,1)S(1)} fusion(f32[2,8,256,2304]{2,3,1,0:T(8,128)} %get-tuple-element.236, f32[2,8,256]{2,1,0:T(8,128)S(1)} %get-tuple-element.237, bf16[256,2,128]{0,2,1:T(8,128)(2,1)S(1)} %bitcast.115, bf16[2048,2,128]{0,2,1:T(8,128)(2,1)S(1)} %copy.57), kind=kOutput, calls=%fused_computation.14.clone.1 | convolution fusion | flops 2437677056 | bytes 39993344 | tf_op jit(solution)/shard_map/while/body/eval_jaxpr/kgnm,mkd->nkgd/dot_general | solution.py:92
  427.7 1.0 constant_dynamic-update-slice_fusion.2
  (58 shorter events, 10.8 us)
Async XLA Ops:
  7.2 23.3 %copy-start.1 = (f32[256,1024]{1,0:T(8,128)S(1)}, f32[256,1024]{1,0:T(8,128)}, u32[]{:S(2)}) copy-start(f32[256,1024]{1,0:T(8,128)} %param.13) | copy-start | bytes 3145732
  7.2 143.0 %all-gather.6.cloned.1.call-start = ((), (), s32[]{:S(2)}) async-start(), calls=%async_computation.4 | async-start | bytes 4718592 | tf_op jit(solution)/shard_map/all_gather | solution.py:55
  30.4 127.7 %all-gather.4.cloned.1.call-start = ((), (), s32[]{:S(2)}) async-start(), calls=%async_computation.3 | async-start | bytes 4718592 | tf_op jit(solution)/shard_map/all_gather | solution.py:56
  48.3 260.4 %all-gather.8.cloned.1.call-start = ((), (), s32[]{:S(2)}) async-start(), calls=%async_computation.5 | async-start | bytes 37748736 | tf_op jit(solution)/shard_map/all_gather | solution.py:54
  148.8 0.7 copy-start.2
  334.9 7.7 %copy-start.3 = (s32[1,2,16]{2,1,0:T(2,128)S(1)}, s32[1,2,16]{2,1,0:T(2,128)}, u32[]{:S(2)}) copy-start(s32[1,2,16]{2,1,0:T(2,128)} %param.17) | copy-start | bytes 388
  338.9 3.7 copy-start
Sparse Core Ops, SparseCore 0:
  30.5 35.6 all-gather.5
  68.7 36.5 all-gather.3
  149.0 159.7 all-gather.7
